TPU v7x, 32 devices: a whole 2x2x4 slice. The times are simulated.
32 devices in a mesh: section: 4 (over y, core), seq: 8 (over z, x).
Axes of the slice: x: 2, y: 2, z: 4, core: 2. Of those that a mesh axis runs over, the one named last changes fastest.
Arguments:
- queries: bfloat16 [4, 1024, 2048], P('section', 'seq'), may hold values from -4 to 4
- memory_keys: bfloat16 [4, 1024, 2048], P('section', 'seq'), may hold values from -2.5 to 2.5
- memory_values: bfloat16 [4, 1024, 2048], P('section', 'seq'), may hold values from -4 to 4
- upstream: bfloat16 [4, 1024, 2048], P('section', 'seq'), may hold values from -4 to 4
- inner_rate: float32 [4, 32], P('section'), may hold values from 0.02 to 0.2
- checkpoints: float32 [4, 8, 32, 4096], P('section', 'seq'), may hold values from -0.75 to 0.75
Outputs:
- grad_queries: bfloat16 [4, 1024, 2048], P('section', 'seq')
- grad_keys: bfloat16 [4, 1024, 2048], P('section', 'seq')
- grad_values: bfloat16 [4, 1024, 2048], P('section', 'seq')
- adjoint_start: float32 [4, 8, 32, 4096], P('section', 'seq')
All inputs are finite; a program needn't handle non-finite values.
Results may differ from a plain program's by a relative error of at most 0.001.
Values may be sent and summed in bfloat16 or wider, within the bound.
A program may use at most 128 MiB of HBM per device.

v0:
```python
from functools import partial

import jax
import jax.numpy as jnp
from jax import lax
from jax.experimental import pallas as pl
from jax.experimental.pallas import tpu as pltpu
from jax.sharding import PartitionSpec as P

MB = 64
LANES = 128
F32 = jnp.float32
BF16 = jnp.bfloat16
MESH = pl.DeviceIdType.MESH


def nn(a, b):
    return lax.dot_general(a, b, (((1,), (0,)), ((), ())), preferred_element_type=F32)


def nt(a, b):
    return lax.dot_general(a, b, (((1,), (1,)), ((), ())), preferred_element_type=F32)


def tn(a, b):
    return lax.dot_general(a, b, (((0,), (0,)), ((), ())), preferred_element_type=F32)


def split(x):
    high = x.astype(BF16)
    return high, (x - high.astype(F32)).astype(BF16)


def stacked(parts):
    return jnp.concatenate(parts, axis=0)


def tiles(x):
    return [x[:, i : i + LANES] for i in range(0, x.shape[1], LANES)]


def diagonal(x, dh):
    per = LANES // dh
    lane = lax.broadcasted_iota(jnp.int32, (x.shape[0], LANES), 1) // dh
    masks = [(lane == i).astype(F32).astype(BF16) for i in range(per)]
    pieces = tiles(x)
    zero = jnp.zeros((x.shape[0], LANES), x.dtype)
    rows = []
    for t, piece in enumerate(pieces):
        for i in range(per):
            row = [zero] * len(pieces)
            row[t] = piece * masks[i]
            rows.append(jnp.concatenate(row, axis=1))
    return stacked(rows)


def folded(a, b, dh):
    per = LANES // dh
    lane = lax.broadcasted_iota(jnp.int32, (dh, LANES), 1) // dh
    out = []
    for left, right in zip(tiles(a), tiles(b)):
        product = tn(left, right)
        value = product[:dh]
        for i in range(1, per):
            value = jnp.where(lane == i, product[i * dh : (i + 1) * dh], value)
        out.append(value)
    return jnp.concatenate(out, axis=1)


def rows_times(x, weights, multiply=nn):
    high, low = split(x)
    both = multiply(stacked([high, low]), weights)
    return both[: x.shape[0]] + both[x.shape[0] :]


def full_times(x, weights, multiply=nn):
    return rows_times(x, weights[0], multiply) + multiply(x.astype(BF16), weights[1])


def halves(x, dh):
    high, low = split(x)
    return diagonal(high, dh), diagonal(low, dh)


def exact_times(x, weights, multiply=nn):
    return multiply(x, weights[0]) + multiply(x, weights[1])


def doubled(a, b):
    return stacked([a, a]), stacked(split(b))


def lane_index(shape, dh):
    return lax.broadcasted_iota(jnp.int32, shape, 1) % dh


def upper_mask(width):
    row = lax.broadcasted_iota(jnp.int32, (MB, width), 0)
    return (lane_index((MB, width), MB) >= row).astype(F32)


def weight_part(k, v, c, w, dh):
    width = c.shape[1]
    row = lax.broadcasted_iota(jnp.int32, (dh, width), 0)
    eye = jnp.where(row == lane_index((dh, width), dh), 1.0, 0.0)
    weights, errors, linear = [], [], []
    for t in range(len(k)):
        e = exact_times(k[t], halves(w, dh)) - v[t].astype(F32)
        yield
        weights.append(w)
        errors.append(e)
        if t + 1 < len(k):
            w = w - c * folded(*doubled(k[t], e), dh)
            yield
        linear.append(eye - c * folded(k[t], k[t], dh))
        yield
    a = linear[-1]
    for t in range(len(k) - 2, -1, -1):
        a = full_times(linear[t], halves(a, dh))
    return weights, errors, a


def interleaved(runs):
    results, waiting = [None] * len(runs), dict(enumerate(runs))
    while waiting:
        for i, run in list(waiting.items()):
            try:
                next(run)
            except StopIteration as stop:
                results[i] = stop.value
                del waiting[i]
    return results


def step_back(q, k, z, error_grad, dh):
    high, low = split(error_grad)
    return folded(stacked([q, k, k]), stacked([z, high, low]), dh)


def source_part(q, k, z, c, dh):
    upper = upper_mask(c.shape[1])
    carried = [None] * len(k)
    for t in range(len(k) - 1, -1, -1):
        scores = nt(k[t], diagonal(q[t], dh)) * upper
        yield
        carried[t] = rows_times(scores, diagonal(z[t], dh))
        yield
    b = None
    for t in range(len(k) - 1, -1, -1):
        total = carried[t] if b is None else carried[t] + exact_times(k[t], halves(b, dh))
        yield
        update = step_back(q[t], k[t], z[t], total * -c, dh)
        b = update if b is None else b + update
        yield
    return carried, b


def score_part(q, k, z, c, weights, errors, dh):
    upper = upper_mask(c.shape[1])
    query_grads, key_part = [], []
    for t in range(len(k)):
        score_grad = rows_times(errors[t], diagonal(z[t], dh), nt) * (upper * -c)
        yield
        key_part.append(rows_times(score_grad, diagonal(q[t], dh)))
        yield
        high, low = split(score_grad)
        query_grads.append(
            exact_times(z[t], halves(weights[t], dh), nt)
            + folded(stacked([high, low]), stacked([k[t], k[t]]), dh)
        )
        yield
    return query_grads, key_part


def final_part(q, k, z, c, weights, errors, carried, key_part, g, dh):
    count = len(q)
    key_grads, value_grads = [None] * count, [None] * count
    for t in range(count - 1, -1, -1):
        whole = halves(g, dh)
        minus = c * (carried[t] + exact_times(k[t], whole))
        yield
        value_grads[t] = minus
        g = g + step_back(q[t], k[t], z[t], -minus, dh)
        yield
        partial_grad = key_part[t] - c * full_times(errors[t], whole, nt)
        yield
        key_grads[t] = partial_grad - full_times(minus, halves(weights[t], dh), nt)
        yield
    return key_grads, value_grads, g


def cut(ref, lanes, size=MB):
    return [ref[i : i + size, lanes] for i in range(0, ref.shape[0], size)]


def put(ref, lanes, parts):
    size = ref.shape[0] // len(parts)
    for i, part in enumerate(parts):
        ref[i * size : (i + 1) * size, lanes] = part.astype(ref.dtype)


def kernel(
    dh, width, upstream, q_in, k_in, v_in, rates, checkpoint,
    gq, gk, gv, rows_of_heads,
    q, k, v, in_sems, stage,
    z, trail, err, car, kp, a, b, other_a, other_b, pair_a, pair_b, second_a, second_b,
    entering, leaving, back, end,
    line_sem, up_sems, a_send, a_recv, b_send, b_recv, g_send, g_recv, r_send, r_recv,
):
    shard, shards = lax.axis_index("seq"), lax.axis_size("seq")
    section, sections = lax.axis_index("section"), lax.axis_size("section")
    features = q.shape[1]
    half = features // 2
    chunks = half // width
    side = lax.rem(shard, 2)
    partner = (section, shard + 1 - 2 * side)
    before = (section, jnp.maximum(shard - 2, 0))
    after = (section, jnp.minimum(shard + 2, shards - 1))
    below = (lax.rem(section + sections - 1, sections), shard)
    above = (lax.rem(section + 1, sections), shard)
    not_first = shard >= 2
    not_last = shard < shards - 2

    loads = [
        pltpu.make_async_copy(x, y, in_sems.at[i])
        for i, (x, y) in enumerate(((k_in, k), (v_in, v), (q_in, q)))
    ]
    for load in loads:
        load.start()

    barrier = pltpu.get_barrier_semaphore()
    for peer in (below, above, partner):
        pl.semaphore_signal(barrier, inc=1, device_id=peer, device_id_type=MESH)
    for present, peer in ((not_first, before), (not_last, after)):
        @pl.when(present)
        def _():
            pl.semaphore_signal(barrier, inc=1, device_id=peer, device_id_type=MESH)
    pl.semaphore_wait(barrier, 3 + not_first.astype(jnp.int32) + not_last.astype(jnp.int32))

    def remote(source, target, send, recv, peer):
        return pltpu.make_async_remote_copy(
            src_ref=source, dst_ref=target, send_sem=send, recv_sem=recv,
            device_id=peer, device_id_type=MESH,
        )

    upward = remote(upstream, z, up_sems.at[0], up_sems.at[1], below)
    upward.start()

    heads = features // dh
    lines = dh * dh // LANES

    def line_in(i):
        return pltpu.make_async_copy(
            checkpoint.at[:, pl.ds(i * LANES, LANES)],
            rows_of_heads.at[pl.ds(i * heads, heads), :],
            line_sem.at[i],
        )

    for i in range(lines):
        line_in(i).start()
    for i in range(lines):
        line_in(i).wait()

    left = lax.broadcasted_iota(jnp.int32, (lines, LANES), 1) < dh

    def swap(x):
        return jnp.concatenate([x[:, dh:], x[:, :dh]], axis=1)

    def head_of(lanes):
        return (lanes.start // LANES) * (LANES // dh)

    def rate_of(lanes):
        head = head_of(lanes)
        first = lax.broadcasted_iota(jnp.int32, (1, LANES), 1) < dh
        return jnp.where(first, rates[0, head], rates[0, head + 1]) / MB

    def load_weight(lanes):
        head = head_of(lanes)
        x = rows_of_heads[pl.ds(head, lines, stride=heads), :]
        y = rows_of_heads[pl.ds(head + 1, lines, stride=heads), :]
        base = head * (dh // 2)
        stage[pl.ds(base, lines, stride=2), :] = jnp.where(left, x, swap(y))
        stage[pl.ds(base + 1, lines, stride=2), :] = jnp.where(left, swap(x), y)
        trail[:dh, lanes] = stage[pl.ds(pl.multiple_of(base, dh), dh), :]

    def store_start(lanes, first):
        head = head_of(lanes)
        base = head * (dh // 2)
        stage[pl.ds(pl.multiple_of(base, dh), dh), :] = first
        even = stage[pl.ds(base, lines, stride=2), :]
        odd = stage[pl.ds(base + 1, lines, stride=2), :]
        rows_of_heads[pl.ds(head, lines, stride=heads), :] = jnp.where(left, even, swap(odd))
        rows_of_heads[pl.ds(head + 1, lines, stride=heads), :] = jnp.where(left, swap(even), odd)

    def own(i):
        return pl.ds(pl.multiple_of(side * half + i * width, width), width)

    def others(i):
        return pl.ds(pl.multiple_of((1 - side) * half + i * width, width), width)

    def place(i):
        return pl.ds(pl.multiple_of(i * width, width), width)

    def send_a(i):
        return remote(a.at[:, others(i)], other_a.at[:, place(i)], a_send.at[i], a_recv.at[i], partner)

    def send_b(i):
        return remote(b.at[:, others(i)], other_b.at[:, place(i)], b_send.at[i], b_recv.at[i], partner)

    def thin(i):
        return pl.ds(pl.multiple_of(i * LANES, LANES), LANES)

    def own_thin(i):
        return pl.ds(pl.multiple_of(side * half + i * LANES, LANES), LANES)

    def others_thin(i):
        return pl.ds(pl.multiple_of((1 - side) * half + i * LANES, LANES), LANES)

    fine = width // LANES

    def send_g(i):
        return remote(leaving.at[:, thin(i)], entering.at[:, thin(i)], g_send.at[i], g_recv.at[i], before)

    def send_r(i):
        return remote(back.at[:, thin(i)], end.at[:, own_thin(i)], r_send.at[i], r_recv.at[i], partner)

    def await_r(i):
        return remote(back.at[:, thin(i)], end.at[:, others_thin(i)], r_send.at[i], r_recv.at[i], partner)

    def narrow(span):
        start_lane = span.start
        return [
            pl.ds(pl.multiple_of(start_lane + j, LANES), LANES) for j in range(0, width, LANES)
        ]

    def together(compute, store, spans):
        groups = [lanes for span in spans for lanes in narrow(span)]
        results = interleaved([compute(lanes) for lanes in groups])
        for lanes, result in zip(groups, results):
            store(lanes, *result)

    def weights_of(lanes):
        return weight_part(cut(k, lanes), cut(v, lanes), rate_of(lanes), trail[:dh, lanes], dh)

    def put_weights(lanes, weights, errors, linear):
        for t in range(1, len(weights)):
            trail[t * dh : (t + 1) * dh, lanes] = weights[t]
        put(err, lanes, errors)
        a[:, lanes] = linear

    def sources_of(lanes):
        return source_part(cut(q, lanes), cut(k, lanes), cut(z, lanes), rate_of(lanes), dh)

    def put_sources(lanes, carried, offset):
        put(car, lanes, carried)
        b[:, lanes] = offset

    def scores_of(lanes):
        return score_part(
            cut(q, lanes), cut(k, lanes), cut(z, lanes), rate_of(lanes),
            cut(trail, lanes, dh), cut(err, lanes), dh,
        )

    def put_scores(lanes, query_grads, key_part):
        put(gq, lanes, query_grads)
        put(kp, lanes, key_part)

    def finals_of(lanes):
        return final_part(
            cut(q, lanes), cut(k, lanes), cut(z, lanes), rate_of(lanes),
            cut(trail, lanes, dh), cut(err, lanes), cut(car, lanes), cut(kp, lanes), end[:, lanes], dh,
        )

    def put_finals(lanes, key_grads, value_grads, first):
        put(gk, lanes, key_grads)
        put(gv, lanes, value_grads)
        store_start(lanes, first)

    def each(body, first=0, last=chunks):
        def step(i, nothing):
            body(i)
            return nothing

        lax.fori_loop(first, last, step, jnp.int32(0))

    def first_step(i):
        for span in (others(i), own(i)):
            for lanes in narrow(span):
                load_weight(lanes)
        together(weights_of, put_weights, [others(i), own(i)])
        send_a(i).start()

    def second_step(i):
        together(sources_of, put_sources, [others(i), own(i)])
        send_b(i).start()

    is_even = side == 0

    def pair_step(i):
        lanes, local = own(i), place(i)
        send_a(i).wait_recv()
        send_b(i).wait_recv()
        near_a, near_b = a[:, lanes], b[:, lanes]
        far_a, far_b = other_a[:, local], other_b[:, local]
        a1 = jnp.where(is_even, far_a, near_a)
        b1 = jnp.where(is_even, far_b, near_b)
        a0 = jnp.where(is_even, near_a, far_a)
        b0 = jnp.where(is_even, near_b, far_b)
        offset = full_times(a0, halves(b1, dh)) + b0
        leaving[:, local] = offset

        @pl.when(not_first & jnp.logical_not(not_last))
        def _():
            for j in range(fine):
                send_g(i * fine + j).start()

        pair_b[:, local] = offset
        pair_a[:, local] = full_times(a0, halves(a1, dh))
        second_a[:, local] = a1
        second_b[:, local] = b1

    def score_step(i):
        together(scores_of, put_scores, [others(i), own(i)])

    def relay_step(i):
        lanes, local = own_thin(i), thin(i)

        @pl.when(not_last)
        def _():
            send_g(i).wait_recv()
            incoming = entering[:, local]
            whole = halves(incoming, dh)
            leaving[:, local] = full_times(pair_a[:, local], whole) + pair_b[:, local]

            @pl.when(not_first)
            def _():
                send_g(i).start()

            middle = full_times(second_a[:, local], whole) + second_b[:, local]
            back[:, local] = jnp.where(is_even, incoming, middle)
            end[:, lanes] = jnp.where(is_even, middle, incoming)

        @pl.when(jnp.logical_not(not_last))
        def _():
            middle = second_b[:, local]
            nothing = jnp.zeros_like(middle)
            back[:, local] = jnp.where(is_even, nothing, middle)
            end[:, lanes] = jnp.where(is_even, middle, nothing)

        send_r(i).start()

    def last_step(i):
        for j in range(fine):
            await_r(i * fine + j).wait_recv()
        together(finals_of, put_finals, [own(i), others(i)])

    def drain(i):
        send_a(i).wait_send()
        send_b(i).wait_send()
        for j in range(fine):
            send_r(i * fine + j).wait_send()

            @pl.when(not_first)
            def _():
                send_g(i * fine + j).wait_send()

    loads[0].wait()
    loads[1].wait()
    each(first_step)
    loads[2].wait()
    upward.wait_recv()
    each(second_step)
    each(pair_step)
    early = jnp.where(shard < shards - 4, chunks, 0)
    each(score_step, 0, early)
    each(relay_step, 0, chunks * fine)
    each(score_step, early, chunks)
    each(last_step)
    each(drain)
    upward.wait_send()


def store_kernel(heads, gq, gk, gv, rows, gq_out, gk_out, gv_out, start_out, sems, line_sem):
    copies = [
        pltpu.make_async_copy(
            rows.at[pl.ds(i * heads, heads), :], start_out.at[:, pl.ds(i * LANES, LANES)], line_sem.at[i]
        )
        for i in range(rows.shape[0] // heads)
    ] + [
        pltpu.make_async_copy(x, y, sems.at[i])
        for i, (x, y) in enumerate(((gq, gq_out), (gk, gk_out), (gv, gv_out)))
    ]
    for copy in copies:
        copy.start()
    for copy in copies:
        copy.wait()


def per_device(queries, memory_keys, memory_values, upstream, inner_rate, checkpoints):
    heads = inner_rate.shape[1]
    features = queries.shape[2]
    dh = features // heads
    tokens = queries.shape[1]
    width = 2 * LANES
    half = features // 2
    chunks = half // width
    count = tokens // MB

    vmem = pl.BlockSpec(memory_space=pltpu.VMEM)
    hbm = pl.BlockSpec(memory_space=pl.ANY)
    kept = pl.BlockSpec(memory_space=pltpu.HBM)
    assert 2 * dh == LANES
    lines = dh * dh // LANES
    tall = jax.ShapeDtypeStruct((tokens, features), BF16)
    held = pltpu.VMEM((tokens, features), BF16)
    whole = pltpu.VMEM((dh, features), F32)
    part = pltpu.VMEM((dh, half), F32)
    rows = pltpu.VMEM((tokens, features), F32)
    gq, gk, gv, start_rows = pl.pallas_call(
        partial(kernel, dh, width),
        in_specs=[kept] * 4 + [pl.BlockSpec(memory_space=pltpu.SMEM), kept],
        out_specs=[vmem] * 4,
        out_shape=[held, held, held, pltpu.VMEM((lines * heads, LANES), F32)],
        scratch_shapes=[held, held, held, pltpu.SemaphoreType.DMA((3,))] + [
            pltpu.VMEM((features // LANES * dh, LANES), F32),
            pltpu.VMEM((tokens, features), BF16),
            pltpu.VMEM((count * dh, features), F32),
            rows, rows, rows,
            whole, whole,
            part, part, part, part, part, part, part, part, part,
            whole,
            pltpu.SemaphoreType.DMA((lines,)),
            pltpu.SemaphoreType.DMA((2,)),
        ] + [pltpu.SemaphoreType.DMA((chunks,))] * 4
        + [pltpu.SemaphoreType.DMA((half // LANES,))] * 4,
        compiler_params=pltpu.CompilerParams(collective_id=0, has_side_effects=True, vmem_limit_bytes=61 * 2**20 + 2**19),
        name="layer_backward",
    )(upstream[0], queries[0], memory_keys[0], memory_values[0], inner_rate, checkpoints[0, 0])
    gq, gk, gv, start = pl.pallas_call(
        partial(store_kernel, heads),
        in_specs=[hbm] * 4,
        out_specs=[hbm] * 4,
        out_shape=[tall, tall, tall, jax.ShapeDtypeStruct((heads, dh * dh), F32)],
        scratch_shapes=[pltpu.SemaphoreType.DMA((3,)), pltpu.SemaphoreType.DMA((lines,))],
        compiler_params=pltpu.CompilerParams(vmem_limit_bytes=2**20),
        name="store_results",
    )(gq, gk, gv, start_rows)
    return gq[None], gk[None], gv[None], start[None, None]


def solution(mesh):
    return jax.shard_map(
        per_device,
        mesh=mesh,
        in_specs=(
            P("section", "seq", None),
            P("section", "seq", None),
            P("section", "seq", None),
            P("section", "seq", None),
            P("section", None),
            P("section", "seq", None, None),
        ),
        out_specs=(
            P("section", "seq", None),
            P("section", "seq", None),
            P("section", "seq", None),
            P("section", "seq", None, None),
        ),
        check_vma=False,
    )
```

profile of v0, /device:TPU:0, one launch (start us, length us, event | category | flops | bytes accessed | tf_op | source)
XLA Modules:
  0.0 39.2 jit_solution(16943989926758531153)
XLA Ops:
  0.6 36.9 %layer_backward.1 = (bf16[128,2048]{1,0:T(8,128)(2,1)S(1)}, bf16[128,2048]{1,0:T(8,128)(2,1)S(1)}, bf16[128,2048]{1,0:T(8,128)(2,1)S(1)}, f32[1024,128]{1,0:T(8,128)S(1)}) custom-call(bf16[128,2048]{1,0:T(8,128)(2,1)} %bitcast.9, bf16[128,2048]{1,0:T(8,128)(2,1)} %bitcast.10, bf16[128,2048]{1,0:T(8,128)(2,1)} %bitcast.11, bf16[128,2048]{1,0:T(8,128)(2,1)} %bitcast.12, ...), custom_call_target="tpu_custom_call" | custom-call | tf_op jit(solution)/shard_map/layer_backward/pallas_call | solution.py:519
  37.5 1.6 %store_results.1 = (bf16[128,2048]{1,0:T(8,128)(2,1)}, bf16[128,2048]{1,0:T(8,128)(2,1)}, bf16[128,2048]{1,0:T(8,128)(2,1)}, f32[32,4096]{1,0:T(8,128)}) custom-call(bf16[128,2048]{1,0:T(8,128)(2,1)S(1)} %get-tuple-element.12.gq, bf16[128,2048]{1,0:T(8,128)(2,1)S(1)} %get-tuple-element.13.gk, bf16[128,2048]{1,0:T(8,128)(2,1)S(1)} %get-tuple-element.14.gv, ...), custom_call_target="tpu_custom_call" | custom-call | tf_op jit(solution)/shard_map/store_results/pallas_call | solution.py:539
where the time goes:
time: 39.4 us; the launch traced here: 39.2 us
  Pallas kernels  38.5 us (98%)
  between operations  0.64 us (2%)
    pallas_call x1, Pallas kernels, per_device(): pl.pallas_call(partial(kernel, dh, width), in_specs=[kept] * 4 + [pl.Bloc...  36.9 us
    pallas_call x1, Pallas kernels, per_device(): pl.pallas_call(partial(store_kernel, heads), in_specs=[hbm] * 4, out_spec...  1.62 us

commit v1 on v0

--- a/solution.py
+++ b/solution.py
@@ -100,10 +100,7 @@
 
 
 def weight_part(k, v, c, w, dh):
-    width = c.shape[1]
-    row = lax.broadcasted_iota(jnp.int32, (dh, width), 0)
-    eye = jnp.where(row == lane_index((dh, width), dh), 1.0, 0.0)
-    weights, errors, linear = [], [], []
+    weights, errors = [], []
     for t in range(len(k)):
         e = exact_times(k[t], halves(w, dh)) - v[t].astype(F32)
         yield
@@ -112,12 +109,32 @@
         if t + 1 < len(k):
             w = w - c * folded(*doubled(k[t], e), dh)
             yield
-        linear.append(eye - c * folded(k[t], k[t], dh))
+    return weights, errors
+
+
+def linear_part(k, c, dh):
+    width = c.shape[1]
+    row = lax.broadcasted_iota(jnp.int32, (dh, width), 0)
+    eye = jnp.where(row == lane_index((dh, width), dh), 1.0, 0.0)
+    linear = []
+    for block in k:
+        linear.append(eye - c * folded(block, block, dh))
         yield
     a = linear[-1]
     for t in range(len(k) - 2, -1, -1):
         a = full_times(linear[t], halves(a, dh))
-    return weights, errors, a
+        yield
+    return a
+
+
+def pair_linear(near, far, is_even, c, dh):
+    near_a = yield from linear_part(near, c, dh)
+    far_a = yield from linear_part(far, c, dh)
+    first = jnp.where(is_even, near_a, far_a)
+    second = jnp.where(is_even, far_a, near_a)
+    both = full_times(first, halves(second, dh))
+    yield
+    return first, second, both
 
 
 def interleaved(runs):
@@ -200,19 +217,24 @@
 
 
 def kernel(
-    dh, width, upstream, q_in, k_in, v_in, rates, checkpoint,
+    dh, unit, upstream, q_in, k_in, v_in, rates, checkpoint,
     gq, gk, gv, rows_of_heads,
     q, k, v, in_sems, stage,
-    z, trail, err, car, kp, a, b, other_a, other_b, pair_a, pair_b, second_a, second_b,
+    z, far_k, trail, err, car, kp, b, other_b, first_a, second_a, pair_a, pair_b, second_b,
     entering, leaving, back, end,
-    line_sem, up_sems, a_send, a_recv, b_send, b_recv, g_send, g_recv, r_send, r_recv,
+    line_sem, up_send, up_recv, k_send, k_recv, b_send, b_recv, g_send, g_recv, r_send, r_recv,
 ):
     shard, shards = lax.axis_index("seq"), lax.axis_size("seq")
     section, sections = lax.axis_index("section"), lax.axis_size("section")
     features = q.shape[1]
     half = features // 2
-    chunks = half // width
+    units = half // unit
+    piece = 2 * LANES
+    pieces = half // piece
+    per_unit = unit // piece
+    fine = piece // LANES
     side = lax.rem(shard, 2)
+    is_even = side == 0
     partner = (section, shard + 1 - 2 * side)
     before = (section, jnp.maximum(shard - 2, 0))
     after = (section, jnp.minimum(shard + 2, shards - 1))
@@ -220,13 +242,25 @@
     above = (lax.rem(section + 1, sections), shard)
     not_first = shard >= 2
     not_last = shard < shards - 2
+    heads = features // dh
+    lines = dh * dh // LANES
+
+    def line_in(i):
+        return pltpu.make_async_copy(
+            checkpoint.at[:, pl.ds(i * LANES, LANES)],
+            rows_of_heads.at[pl.ds(i * heads, heads), :],
+            line_sem.at[i],
+        )
 
     loads = [
         pltpu.make_async_copy(x, y, in_sems.at[i])
         for i, (x, y) in enumerate(((k_in, k), (v_in, v), (q_in, q)))
     ]
-    for load in loads:
-        load.start()
+    loads[0].start()
+    for i in range(lines):
+        line_in(i).start()
+    loads[1].start()
+    loads[2].start()
 
     barrier = pltpu.get_barrier_semaphore()
     for peer in (below, above, partner):
@@ -235,31 +269,12 @@
         @pl.when(present)
         def _():
             pl.semaphore_signal(barrier, inc=1, device_id=peer, device_id_type=MESH)
-    pl.semaphore_wait(barrier, 3 + not_first.astype(jnp.int32) + not_last.astype(jnp.int32))
 
     def remote(source, target, send, recv, peer):
         return pltpu.make_async_remote_copy(
             src_ref=source, dst_ref=target, send_sem=send, recv_sem=recv,
             device_id=peer, device_id_type=MESH,
         )
-
-    upward = remote(upstream, z, up_sems.at[0], up_sems.at[1], below)
-    upward.start()
-
-    heads = features // dh
-    lines = dh * dh // LANES
-
-    def line_in(i):
-        return pltpu.make_async_copy(
-            checkpoint.at[:, pl.ds(i * LANES, LANES)],
-            rows_of_heads.at[pl.ds(i * heads, heads), :],
-            line_sem.at[i],
-        )
-
-    for i in range(lines):
-        line_in(i).start()
-    for i in range(lines):
-        line_in(i).wait()
 
     left = lax.broadcasted_iota(jnp.int32, (lines, LANES), 1) < dh
 
@@ -292,61 +307,65 @@
         rows_of_heads[pl.ds(head, lines, stride=heads), :] = jnp.where(left, even, swap(odd))
         rows_of_heads[pl.ds(head + 1, lines, stride=heads), :] = jnp.where(left, swap(even), odd)
 
-    def own(i):
-        return pl.ds(pl.multiple_of(side * half + i * width, width), width)
-
-    def others(i):
-        return pl.ds(pl.multiple_of((1 - side) * half + i * width, width), width)
-
-    def place(i):
-        return pl.ds(pl.multiple_of(i * width, width), width)
-
-    def send_a(i):
-        return remote(a.at[:, others(i)], other_a.at[:, place(i)], a_send.at[i], a_recv.at[i], partner)
+    def span(start, size):
+        return pl.ds(pl.multiple_of(start, size), size)
+
+    def own(i, size):
+        return span(side * half + i * size, size)
+
+    def others(i, size):
+        return span((1 - side) * half + i * size, size)
+
+    def place(i, size):
+        return span(i * size, size)
+
+    def send_up(i):
+        lanes = span(lax.rem(1 - side + i // pieces, 2) * half + lax.rem(i, pieces) * piece, piece)
+        return remote(upstream.at[:, lanes], z.at[:, lanes], up_send.at[i], up_recv.at[i], below)
+
+    def send_k(i):
+        return remote(
+            k_in.at[:, others(i, piece)], far_k.at[:, place(i, piece)], k_send.at[i], k_recv.at[i], partner
+        )
 
     def send_b(i):
-        return remote(b.at[:, others(i)], other_b.at[:, place(i)], b_send.at[i], b_recv.at[i], partner)
-
-    def thin(i):
-        return pl.ds(pl.multiple_of(i * LANES, LANES), LANES)
-
-    def own_thin(i):
-        return pl.ds(pl.multiple_of(side * half + i * LANES, LANES), LANES)
-
-    def others_thin(i):
-        return pl.ds(pl.multiple_of((1 - side) * half + i * LANES, LANES), LANES)
-
-    fine = width // LANES
+        return remote(
+            b.at[:, others(i, piece)], other_b.at[:, place(i, piece)], b_send.at[i], b_recv.at[i], partner
+        )
 
     def send_g(i):
-        return remote(leaving.at[:, thin(i)], entering.at[:, thin(i)], g_send.at[i], g_recv.at[i], before)
+        return remote(
+            leaving.at[:, place(i, LANES)], entering.at[:, place(i, LANES)], g_send.at[i], g_recv.at[i], before
+        )
 
     def send_r(i):
-        return remote(back.at[:, thin(i)], end.at[:, own_thin(i)], r_send.at[i], r_recv.at[i], partner)
+        return remote(
+            back.at[:, place(i, LANES)], end.at[:, own(i, LANES)], r_send.at[i], r_recv.at[i], partner
+        )
 
     def await_r(i):
-        return remote(back.at[:, thin(i)], end.at[:, others_thin(i)], r_send.at[i], r_recv.at[i], partner)
-
-    def narrow(span):
-        start_lane = span.start
+        return remote(
+            back.at[:, place(i, LANES)], end.at[:, others(i, LANES)], r_send.at[i], r_recv.at[i], partner
+        )
+
+    def narrow(lanes):
         return [
-            pl.ds(pl.multiple_of(start_lane + j, LANES), LANES) for j in range(0, width, LANES)
+            pl.ds(pl.multiple_of(lanes.start + j, LANES), LANES) for j in range(0, lanes.size, LANES)
         ]
 
-    def together(compute, store, spans):
-        groups = [lanes for span in spans for lanes in narrow(span)]
-        results = interleaved([compute(lanes) for lanes in groups])
-        for lanes, result in zip(groups, results):
-            store(lanes, *result)
+    def together(compute, store, lanes):
+        groups = narrow(lanes)
+        results = interleaved([compute(x) for x in groups])
+        for x, result in zip(groups, results):
+            store(x, *result)
 
     def weights_of(lanes):
         return weight_part(cut(k, lanes), cut(v, lanes), rate_of(lanes), trail[:dh, lanes], dh)
 
-    def put_weights(lanes, weights, errors, linear):
+    def put_weights(lanes, weights, errors):
         for t in range(1, len(weights)):
             trail[t * dh : (t + 1) * dh, lanes] = weights[t]
         put(err, lanes, errors)
-        a[:, lanes] = linear
 
     def sources_of(lanes):
         return source_part(cut(q, lanes), cut(k, lanes), cut(z, lanes), rate_of(lanes), dh)
@@ -376,64 +395,83 @@
         put(gv, lanes, value_grads)
         store_start(lanes, first)
 
-    def each(body, first=0, last=chunks):
+    def each(body, first, last):
         def step(i, nothing):
             body(i)
             return nothing
 
         lax.fori_loop(first, last, step, jnp.int32(0))
 
-    def first_step(i):
-        for span in (others(i), own(i)):
-            for lanes in narrow(span):
-                load_weight(lanes)
-        together(weights_of, put_weights, [others(i), own(i)])
-        send_a(i).start()
-
-    def second_step(i):
-        together(sources_of, put_sources, [others(i), own(i)])
-        send_b(i).start()
-
-    is_even = side == 0
+    def weight_step(i):
+        lanes = span(i * unit, unit)
+        for x in narrow(lanes):
+            load_weight(x)
+        together(weights_of, put_weights, lanes)
+
+    def linear_step(i):
+        for j in range(per_unit):
+            send_k(i * per_unit + j).wait_recv()
+        lanes = own(i, unit)
+        offset = side * half
+
+        def compute(x):
+            local = pl.ds(pl.multiple_of(x.start - offset, LANES), LANES)
+            return pair_linear(cut(k, x), cut(far_k, local), is_even, rate_of(x), dh)
+
+        def store(x, first, second, both):
+            local = pl.ds(pl.multiple_of(x.start - offset, LANES), LANES)
+            first_a[:, local] = first
+            second_a[:, local] = second
+            pair_a[:, local] = both
+
+        together(compute, store, lanes)
+
+    def source_step(i):
+        for j in range(per_unit):
+            send_up(i * per_unit + j).wait_recv()
+        lanes = span(lax.rem(1 - side + i // units, 2) * half + lax.rem(i, units) * unit, unit)
+        together(sources_of, put_sources, lanes)
+
+        @pl.when(i < units)
+        def _():
+            for j in range(per_unit):
+                send_b(i * per_unit + j).start()
+
+        @pl.when((i >= units - 1) & (i < 2 * units - 1))
+        def _():
+            linear_step(i - (units - 1))
 
     def pair_step(i):
-        lanes, local = own(i), place(i)
-        send_a(i).wait_recv()
+        lanes, local = own(i, piece), place(i, piece)
         send_b(i).wait_recv()
-        near_a, near_b = a[:, lanes], b[:, lanes]
-        far_a, far_b = other_a[:, local], other_b[:, local]
-        a1 = jnp.where(is_even, far_a, near_a)
+        near_b, far_b = b[:, lanes], other_b[:, local]
         b1 = jnp.where(is_even, far_b, near_b)
-        a0 = jnp.where(is_even, near_a, far_a)
         b0 = jnp.where(is_even, near_b, far_b)
-        offset = full_times(a0, halves(b1, dh)) + b0
-        leaving[:, local] = offset
+        offset = full_times(first_a[:, local], halves(b1, dh)) + b0
+        pair_b[:, local] = offset
+        second_b[:, local] = b1
 
         @pl.when(not_first & jnp.logical_not(not_last))
         def _():
+            leaving[:, local] = offset
             for j in range(fine):
                 send_g(i * fine + j).start()
 
-        pair_b[:, local] = offset
-        pair_a[:, local] = full_times(a0, halves(a1, dh))
-        second_a[:, local] = a1
-        second_b[:, local] = b1
-
-    def score_step(i):
-        together(scores_of, put_scores, [others(i), own(i)])
+    sends_back = not_last | jnp.logical_not(is_even)
+    gets_back = not_last | is_even
 
     def relay_step(i):
-        lanes, local = own_thin(i), thin(i)
+        lanes, local = own(i, LANES), place(i, LANES)
 
         @pl.when(not_last)
         def _():
             send_g(i).wait_recv()
             incoming = entering[:, local]
             whole = halves(incoming, dh)
-            leaving[:, local] = full_times(pair_a[:, local], whole) + pair_b[:, local]
 
             @pl.when(not_first)
             def _():
+                leaving[:, local] = full_times(pair_a[:, local], whole) + pair_b[:, local]
                 send_g(i).start()
 
             middle = full_times(second_a[:, local], whole) + second_b[:, local]
@@ -444,40 +482,89 @@
         def _():
             middle = second_b[:, local]
             nothing = jnp.zeros_like(middle)
-            back[:, local] = jnp.where(is_even, nothing, middle)
             end[:, lanes] = jnp.where(is_even, middle, nothing)
 
-        send_r(i).start()
+            @pl.when(jnp.logical_not(is_even))
+            def _():
+                back[:, local] = middle
+                end[:, others(i, LANES)] = nothing
+
+        @pl.when(sends_back)
+        def _():
+            send_r(i).start()
+
+    def lanes_of(i):
+        return span(lax.rem(side + i, 2) * half + (i // 2) * unit, unit)
+
+    def score_step(i):
+        together(scores_of, put_scores, lanes_of(i))
 
     def last_step(i):
+        @pl.when((lax.rem(i, 2) == 1) & gets_back)
+        def _():
+            for j in range(unit // LANES):
+                await_r((i // 2) * (unit // LANES) + j).wait_recv()
+
+        together(finals_of, put_finals, lanes_of(i))
+
+    for i in range(lines):
+        line_in(i).wait()
+    loads[0].wait()
+    loads[1].wait()
+    each(weight_step, 0, 1)
+    pl.semaphore_wait(barrier, 3 + not_first.astype(jnp.int32) + not_last.astype(jnp.int32))
+    for i in range(pieces):
+        send_up(i).start()
+        send_k(i).start()
+    for i in range(pieces, 2 * pieces):
+        send_up(i).start()
+    each(weight_step, 1, 2 * units)
+    loads[2].wait()
+    each(source_step, 0, 2 * units)
+
+    distance = (shards - 1 - shard) // 2
+    relay_at = jnp.where(distance == 0, 0, jnp.where(distance == 1, pieces - 1, pieces + 1))
+    early = jnp.where(not_first, 0, 1)
+    total = 2 * units
+
+    def slot(n):
+        @pl.when(n < pieces)
+        def _():
+            pair_step(n)
+
+        @pl.when((n >= relay_at) & (n < relay_at + pieces))
+        def _():
+            for j in range(fine):
+                relay_step((n - relay_at) * fine + j)
+
+        @pl.when((n >= 1) & (n <= total))
+        def _():
+            score_step(n - 1)
+
+        now = n - relay_at
+        index = jnp.where((early == 1) & (now == 1), 0, now - 3 + early)
+
+        @pl.when((index >= early * (now >= 3).astype(jnp.int32)) & (index < total) & ((now >= 3) | (early == 1)) & (now != 2) & (now >= 1))
+        def _():
+            last_step(index)
+
+    each(slot, 0, relay_at + 3 + total)
+
+    def drain(i):
+        send_k(i).wait_send()
+        send_b(i).wait_send()
+        for j in range(2):
+            send_up(i * 2 + j).wait_send()
         for j in range(fine):
-            await_r(i * fine + j).wait_recv()
-        together(finals_of, put_finals, [own(i), others(i)])
-
-    def drain(i):
-        send_a(i).wait_send()
-        send_b(i).wait_send()
-        for j in range(fine):
-            send_r(i * fine + j).wait_send()
+            @pl.when(sends_back)
+            def _():
+                send_r(i * fine + j).wait_send()
 
             @pl.when(not_first)
             def _():
                 send_g(i * fine + j).wait_send()
 
-    loads[0].wait()
-    loads[1].wait()
-    each(first_step)
-    loads[2].wait()
-    upward.wait_recv()
-    each(second_step)
-    each(pair_step)
-    early = jnp.where(shard < shards - 4, chunks, 0)
-    each(score_step, 0, early)
-    each(relay_step, 0, chunks * fine)
-    each(score_step, early, chunks)
-    each(last_step)
-    each(drain)
-    upward.wait_send()
+    each(drain, 0, pieces)
 
 
 def store_kernel(heads, gq, gk, gv, rows, gq_out, gk_out, gv_out, start_out, sems, line_sem):
@@ -501,9 +588,9 @@
     features = queries.shape[2]
     dh = features // heads
     tokens = queries.shape[1]
-    width = 2 * LANES
     half = features // 2
-    chunks = half // width
+    unit = min(4 * LANES, half)
+    pieces = half // (2 * LANES)
     count = tokens // MB
 
     vmem = pl.BlockSpec(memory_space=pltpu.VMEM)
@@ -517,21 +604,23 @@
     part = pltpu.VMEM((dh, half), F32)
     rows = pltpu.VMEM((tokens, features), F32)
     gq, gk, gv, start_rows = pl.pallas_call(
-        partial(kernel, dh, width),
+        partial(kernel, dh, unit),
         in_specs=[kept] * 4 + [pl.BlockSpec(memory_space=pltpu.SMEM), kept],
         out_specs=[vmem] * 4,
         out_shape=[held, held, held, pltpu.VMEM((lines * heads, LANES), F32)],
         scratch_shapes=[held, held, held, pltpu.SemaphoreType.DMA((3,))] + [
             pltpu.VMEM((features // LANES * dh, LANES), F32),
-            pltpu.VMEM((tokens, features), BF16),
+            held,
+            pltpu.VMEM((tokens, half), BF16),
             pltpu.VMEM((count * dh, features), F32),
             rows, rows, rows,
-            whole, whole,
-            part, part, part, part, part, part, part, part, part,
+            whole,
+            part, part, part, part, part, part,
+            part, part, part,
             whole,
             pltpu.SemaphoreType.DMA((lines,)),
-            pltpu.SemaphoreType.DMA((2,)),
-        ] + [pltpu.SemaphoreType.DMA((chunks,))] * 4
+        ] + [pltpu.SemaphoreType.DMA((2 * pieces,))] * 2
+        + [pltpu.SemaphoreType.DMA((pieces,))] * 4
         + [pltpu.SemaphoreType.DMA((half // LANES,))] * 4,
         compiler_params=pltpu.CompilerParams(collective_id=0, has_side_effects=True, vmem_limit_bytes=61 * 2**20 + 2**19),
         name="layer_backward",

time: 39.4 us -> 38.8 us (0.985)
  Pallas kernels: 38.5 us -> 38 us
    pallas_call x1, Pallas kernels: 36.9 us -> 36.4 us  [per_device(): pl.pallas_call(partial(kernel, dh, unit), in_specs=[kept] * 4 + [pl.Block...]
where the time goes in v1:
time: 38.8 us; the launch traced here: 38.7 us
  Pallas kernels  38 us (98%)
  between operations  0.64 us (2%)
    pallas_call x1, Pallas kernels, per_device(): pl.pallas_call(partial(kernel, dh, unit), in_specs=[kept] * 4 + [pl.Block...  36.4 us
    pallas_call x1, Pallas kernels, per_device(): pl.pallas_call(partial(store_kernel, heads), in_specs=[hbm] * 4, out_spec...  1.62 us

profile of v1, /device:TPU:0, one launch (start us, length us, event | category | flops | bytes accessed | tf_op | source)
XLA Modules:
  0.0 38.7 jit_solution(2591564710720430579)
XLA Ops:
  0.6 36.4 %layer_backward.1 = (bf16[128,2048]{1,0:T(8,128)(2,1)S(1)}, bf16[128,2048]{1,0:T(8,128)(2,1)S(1)}, bf16[128,2048]{1,0:T(8,128)(2,1)S(1)}, f32[1024,128]{1,0:T(8,128)S(1)}) custom-call(bf16[128,2048]{1,0:T(8,128)(2,1)} %bitcast.9, bf16[128,2048]{1,0:T(8,128)(2,1)} %bitcast.10, bf16[128,2048]{1,0:T(8,128)(2,1)} %bitcast.11, bf16[128,2048]{1,0:T(8,128)(2,1)} %bitcast.12, ...), custom_call_target="tpu_custom_call" | custom-call | tf_op jit(solution)/shard_map/layer_backward/pallas_call | solution.py:606
  37.1 1.6 %store_results.1 = (bf16[128,2048]{1,0:T(8,128)(2,1)}, bf16[128,2048]{1,0:T(8,128)(2,1)}, bf16[128,2048]{1,0:T(8,128)(2,1)}, f32[32,4096]{1,0:T(8,128)}) custom-call(bf16[128,2048]{1,0:T(8,128)(2,1)S(1)} %get-tuple-element.12.gq, bf16[128,2048]{1,0:T(8,128)(2,1)S(1)} %get-tuple-element.13.gk, bf16[128,2048]{1,0:T(8,128)(2,1)S(1)} %get-tuple-element.14.gv, ...), custom_call_target="tpu_custom_call" | custom-call | tf_op jit(solution)/shard_map/store_results/pallas_call | solution.py:628

commit v2 on v1

--- a/solution.py
+++ b/solution.py
@@ -249,7 +249,7 @@
         return pltpu.make_async_copy(
             checkpoint.at[:, pl.ds(i * LANES, LANES)],
             rows_of_heads.at[pl.ds(i * heads, heads), :],
-            line_sem.at[i],
+            line_sem,
         )
 
     loads = [
@@ -319,34 +319,43 @@
     def place(i, size):
         return span(i * size, size)
 
+    def source_lanes(i):
+        return span(lax.rem(1 - side + i, 2) * half + (i // 2) * unit, unit)
+
     def send_up(i):
-        lanes = span(lax.rem(1 - side + i // pieces, 2) * half + lax.rem(i, pieces) * piece, piece)
-        return remote(upstream.at[:, lanes], z.at[:, lanes], up_send.at[i], up_recv.at[i], below)
+        start = source_lanes(i // per_unit).start + lax.rem(i, per_unit) * piece
+        lanes = span(start, piece)
+        return remote(upstream.at[:, lanes], z.at[:, lanes], up_send, up_recv.at[i], below)
 
     def send_k(i):
         return remote(
-            k_in.at[:, others(i, piece)], far_k.at[:, place(i, piece)], k_send.at[i], k_recv.at[i], partner
+            k_in.at[:, others(i, piece)], far_k.at[:, place(i, piece)], k_send, k_recv.at[i], partner
         )
 
     def send_b(i):
         return remote(
-            b.at[:, others(i, piece)], other_b.at[:, place(i, piece)], b_send.at[i], b_recv.at[i], partner
+            b.at[:, others(i, piece)], other_b.at[:, place(i, piece)], b_send, b_recv.at[i], partner
         )
 
     def send_g(i):
         return remote(
-            leaving.at[:, place(i, LANES)], entering.at[:, place(i, LANES)], g_send.at[i], g_recv.at[i], before
-        )
-
-    def send_r(i):
+            leaving.at[:, place(i, LANES)], entering.at[:, place(i, LANES)], g_send, g_recv.at[i], before
+        )
+
+    def send_r(i, source):
         return remote(
-            back.at[:, place(i, LANES)], end.at[:, own(i, LANES)], r_send.at[i], r_recv.at[i], partner
+            source.at[:, place(i, LANES)], end.at[:, own(i, LANES)], r_send, r_recv.at[i], partner
         )
 
     def await_r(i):
         return remote(
-            back.at[:, place(i, LANES)], end.at[:, others(i, LANES)], r_send.at[i], r_recv.at[i], partner
-        )
+            back.at[:, place(i, LANES)], end.at[:, others(i, LANES)], r_send, r_recv.at[i], partner
+        )
+
+    sends_k = not_last | is_even
+    gets_k = not_last | jnp.logical_not(is_even)
+    sends_back = not_last | jnp.logical_not(is_even)
+    gets_back = not_last | is_even
 
     def narrow(lanes):
         return [
@@ -409,8 +418,11 @@
         together(weights_of, put_weights, lanes)
 
     def linear_step(i):
-        for j in range(per_unit):
-            send_k(i * per_unit + j).wait_recv()
+        @pl.when(gets_k)
+        def _():
+            for j in range(per_unit):
+                send_k(i * per_unit + j).wait_recv()
+
         lanes = own(i, unit)
         offset = side * half
 
@@ -429,17 +441,7 @@
     def source_step(i):
         for j in range(per_unit):
             send_up(i * per_unit + j).wait_recv()
-        lanes = span(lax.rem(1 - side + i // units, 2) * half + lax.rem(i, units) * unit, unit)
-        together(sources_of, put_sources, lanes)
-
-        @pl.when(i < units)
-        def _():
-            for j in range(per_unit):
-                send_b(i * per_unit + j).start()
-
-        @pl.when((i >= units - 1) & (i < 2 * units - 1))
-        def _():
-            linear_step(i - (units - 1))
+        together(sources_of, put_sources, source_lanes(i))
 
     def pair_step(i):
         lanes, local = own(i, piece), place(i, piece)
@@ -457,15 +459,17 @@
             for j in range(fine):
                 send_g(i * fine + j).start()
 
-    sends_back = not_last | jnp.logical_not(is_even)
-    gets_back = not_last | is_even
-
     def relay_step(i):
         lanes, local = own(i, LANES), place(i, LANES)
 
         @pl.when(not_last)
         def _():
             send_g(i).wait_recv()
+
+            @pl.when(is_even)
+            def _():
+                send_r(i, entering).start()
+
             incoming = entering[:, local]
             whole = halves(incoming, dh)
 
@@ -475,8 +479,12 @@
                 send_g(i).start()
 
             middle = full_times(second_a[:, local], whole) + second_b[:, local]
-            back[:, local] = jnp.where(is_even, incoming, middle)
             end[:, lanes] = jnp.where(is_even, middle, incoming)
+
+            @pl.when(jnp.logical_not(is_even))
+            def _():
+                back[:, local] = middle
+                send_r(i, back).start()
 
         @pl.when(jnp.logical_not(not_last))
         def _():
@@ -488,10 +496,7 @@
             def _():
                 back[:, local] = middle
                 end[:, others(i, LANES)] = nothing
-
-        @pl.when(sends_back)
-        def _():
-            send_r(i).start()
+                send_r(i, back).start()
 
     def lanes_of(i):
         return span(lax.rem(side + i, 2) * half + (i // 2) * unit, unit)
@@ -507,73 +512,94 @@
 
         together(finals_of, put_finals, lanes_of(i))
 
-    for i in range(lines):
-        line_in(i).wait()
+    pl.semaphore_wait(barrier, 3 + not_first.astype(jnp.int32) + not_last.astype(jnp.int32))
+    for i in range(2 * pieces):
+        send_up(i).start()
+
+    @pl.when(sends_k)
+    def _():
+        for i in range(pieces):
+            send_k(i).start()
+
+    pltpu.make_async_copy(rows_of_heads, rows_of_heads, line_sem).wait()
     loads[0].wait()
     loads[1].wait()
-    each(weight_step, 0, 1)
-    pl.semaphore_wait(barrier, 3 + not_first.astype(jnp.int32) + not_last.astype(jnp.int32))
-    for i in range(pieces):
-        send_up(i).start()
-        send_k(i).start()
-    for i in range(pieces, 2 * pieces):
-        send_up(i).start()
-    each(weight_step, 1, 2 * units)
+    each(weight_step, 0, 2 * units)
     loads[2].wait()
-    each(source_step, 0, 2 * units)
+    total = 2 * units
+
+    def advance(n):
+        even_slot = lax.rem(n, 2) == 0
+
+        @pl.when(n < total)
+        def _():
+            source_step(n)
+
+        @pl.when(even_slot & (n < total))
+        def _():
+            for j in range(per_unit):
+                send_b((n // 2) * per_unit + j).start()
+
+        @pl.when(even_slot & (n >= 2))
+        def _():
+            for j in range(per_unit):
+                pair_step((n // 2 - 1) * per_unit + j)
+
+        @pl.when(even_slot & (n < total))
+        def _():
+            linear_step(n // 2)
+
+    each(advance, 0, total + 1)
 
     distance = (shards - 1 - shard) // 2
-    relay_at = jnp.where(distance == 0, 0, jnp.where(distance == 1, pieces - 1, pieces + 1))
+    near = distance == 1
+    relay_at = jnp.where(distance == 0, 0, jnp.where(near, 1, total))
     early = jnp.where(not_first, 0, 1)
-    total = 2 * units
 
     def slot(n):
-        @pl.when(n < pieces)
-        def _():
-            pair_step(n)
-
-        @pl.when((n >= relay_at) & (n < relay_at + pieces))
+        now = n - relay_at
+
+        @pl.when((now >= 0) & (now < pieces))
         def _():
             for j in range(fine):
-                relay_step((n - relay_at) * fine + j)
-
-        @pl.when((n >= 1) & (n <= total))
-        def _():
-            score_step(n - 1)
-
-        now = n - relay_at
-        index = jnp.where((early == 1) & (now == 1), 0, now - 3 + early)
-
-        @pl.when((index >= early * (now >= 3).astype(jnp.int32)) & (index < total) & ((now >= 3) | (early == 1)) & (now != 2) & (now >= 1))
+                relay_step(now * fine + j)
+
+        chosen = jnp.where(near, (n + 1) // 2, n)
+
+        @pl.when((chosen < total) & (jnp.logical_not(near) | ((n != 1) & (n != 3))))
+        def _():
+            score_step(chosen)
+
+        index = jnp.where(now == 1, 0, now - 3 + early)
+
+        @pl.when((index < total) & ((now >= 3) | ((now == 1) & (early == 1))))
         def _():
             last_step(index)
 
     each(slot, 0, relay_at + 3 + total)
 
-    def drain(i):
-        send_k(i).wait_send()
-        send_b(i).wait_send()
-        for j in range(2):
-            send_up(i * 2 + j).wait_send()
-        for j in range(fine):
-            @pl.when(sends_back)
-            def _():
-                send_r(i * fine + j).wait_send()
-
-            @pl.when(not_first)
-            def _():
-                send_g(i * fine + j).wait_send()
-
-    each(drain, 0, pieces)
+    remote(upstream, z, up_send, up_recv.at[0], below).wait_send()
+    remote(b.at[:, others(0, half)], other_b, b_send, b_recv.at[0], partner).wait_send()
+
+    @pl.when(sends_k)
+    def _():
+        remote(k_in.at[:, others(0, half)], far_k, k_send, k_recv.at[0], partner).wait_send()
+
+    @pl.when(sends_back)
+    def _():
+        remote(back, end.at[:, own(0, half)], r_send, r_recv.at[0], partner).wait_send()
+
+    @pl.when(not_first)
+    def _():
+        remote(leaving, entering, g_send, g_recv.at[0], before).wait_send()
 
 
 def store_kernel(heads, gq, gk, gv, rows, gq_out, gk_out, gv_out, start_out, sems, line_sem):
+    for i in range(rows.shape[0] // heads):
+        pltpu.make_async_copy(
+            rows.at[pl.ds(i * heads, heads), :], start_out.at[:, pl.ds(i * LANES, LANES)], line_sem
+        ).start()
     copies = [
-        pltpu.make_async_copy(
-            rows.at[pl.ds(i * heads, heads), :], start_out.at[:, pl.ds(i * LANES, LANES)], line_sem.at[i]
-        )
-        for i in range(rows.shape[0] // heads)
-    ] + [
         pltpu.make_async_copy(x, y, sems.at[i])
         for i, (x, y) in enumerate(((gq, gq_out), (gk, gk_out), (gv, gv_out)))
     ]
@@ -581,6 +607,7 @@
         copy.start()
     for copy in copies:
         copy.wait()
+    pltpu.make_async_copy(rows, rows, line_sem).wait()
 
 
 def per_device(queries, memory_keys, memory_values, upstream, inner_rate, checkpoints):
@@ -618,10 +645,10 @@
             part, part, part, part, part, part,
             part, part, part,
             whole,
-            pltpu.SemaphoreType.DMA((lines,)),
-        ] + [pltpu.SemaphoreType.DMA((2 * pieces,))] * 2
-        + [pltpu.SemaphoreType.DMA((pieces,))] * 4
-        + [pltpu.SemaphoreType.DMA((half // LANES,))] * 4,
+            pltpu.SemaphoreType.DMA,
+            pltpu.SemaphoreType.DMA, pltpu.SemaphoreType.DMA((2 * pieces,)),
+        ] + [pltpu.SemaphoreType.DMA, pltpu.SemaphoreType.DMA((pieces,))] * 2
+        + [pltpu.SemaphoreType.DMA, pltpu.SemaphoreType.DMA((half // LANES,))] * 2,
         compiler_params=pltpu.CompilerParams(collective_id=0, has_side_effects=True, vmem_limit_bytes=61 * 2**20 + 2**19),
         name="layer_backward",
     )(upstream[0], queries[0], memory_keys[0], memory_values[0], inner_rate, checkpoints[0, 0])
@@ -630,7 +657,7 @@
         in_specs=[hbm] * 4,
         out_specs=[hbm] * 4,
         out_shape=[tall, tall, tall, jax.ShapeDtypeStruct((heads, dh * dh), F32)],
-        scratch_shapes=[pltpu.SemaphoreType.DMA((3,)), pltpu.SemaphoreType.DMA((lines,))],
+        scratch_shapes=[pltpu.SemaphoreType.DMA((3,)), pltpu.SemaphoreType.DMA],
         compiler_params=pltpu.CompilerParams(vmem_limit_bytes=2**20),
         name="store_results",
     )(gq, gk, gv, start_rows)

time: 38.8 us -> 37.7 us (0.972)
  Pallas kernels: 38 us -> 36.9 us
    pallas_call x1, Pallas kernels: 36.4 us -> 35.6 us  [per_device(): pl.pallas_call(partial(kernel, dh, unit), in_specs=[kept] * 4 + [pl.Block...]
where the time goes in v2:
time: 37.7 us; the launch traced here: 37.6 us
  Pallas kernels  36.9 us (98%)
  between operations  0.64 us (2%)
    pallas_call x1, Pallas kernels, per_device(): pl.pallas_call(partial(kernel, dh, unit), in_specs=[kept] * 4 + [pl.Block...  35.6 us
    pallas_call x1, Pallas kernels, per_device(): pl.pallas_call(partial(store_kernel, heads), in_specs=[hbm] * 4, out_spec...  1.35 us

profile of v2, /device:TPU:0, one launch (start us, length us, event | category | flops | bytes accessed | tf_op | source)
XLA Modules:
  0.0 37.6 jit_solution(2049397891101395827)
XLA Ops:
  0.6 35.6 %layer_backward.1 = (bf16[128,2048]{1,0:T(8,128)(2,1)S(1)}, bf16[128,2048]{1,0:T(8,128)(2,1)S(1)}, bf16[128,2048]{1,0:T(8,128)(2,1)S(1)}, f32[1024,128]{1,0:T(8,128)S(1)}) custom-call(bf16[128,2048]{1,0:T(8,128)(2,1)} %bitcast.9, bf16[128,2048]{1,0:T(8,128)(2,1)} %bitcast.10, bf16[128,2048]{1,0:T(8,128)(2,1)} %bitcast.11, bf16[128,2048]{1,0:T(8,128)(2,1)} %bitcast.12, ...), custom_call_target="tpu_custom_call" | custom-call | tf_op jit(solution)/shard_map/layer_backward/pallas_call | solution.py:633
  36.2 1.3 %store_results.1 = (bf16[128,2048]{1,0:T(8,128)(2,1)}, bf16[128,2048]{1,0:T(8,128)(2,1)}, bf16[128,2048]{1,0:T(8,128)(2,1)}, f32[32,4096]{1,0:T(8,128)}) custom-call(bf16[128,2048]{1,0:T(8,128)(2,1)S(1)} %get-tuple-element.12.gq, bf16[128,2048]{1,0:T(8,128)(2,1)S(1)} %get-tuple-element.13.gk, bf16[128,2048]{1,0:T(8,128)(2,1)S(1)} %get-tuple-element.14.gv, ...), custom_call_target="tpu_custom_call" | custom-call | tf_op jit(solution)/shard_map/store_results/pallas_call | solution.py:655

commit v3 on v2

--- a/solution.py
+++ b/solution.py
@@ -320,7 +320,7 @@
         return span(i * size, size)
 
     def source_lanes(i):
-        return span(lax.rem(1 - side + i, 2) * half + (i // 2) * unit, unit)
+        return span(lax.rem(1 - side + i // units, 2) * half + lax.rem(i, units) * unit, unit)
 
     def send_up(i):
         start = source_lanes(i // per_unit).start + lax.rem(i, per_unit) * piece
@@ -499,16 +499,16 @@
                 send_r(i, back).start()
 
     def lanes_of(i):
-        return span(lax.rem(side + i, 2) * half + (i // 2) * unit, unit)
+        return span(lax.rem(side + i // units, 2) * half + lax.rem(i, units) * unit, unit)
 
     def score_step(i):
         together(scores_of, put_scores, lanes_of(i))
 
     def last_step(i):
-        @pl.when((lax.rem(i, 2) == 1) & gets_back)
+        @pl.when((i >= units) & gets_back)
         def _():
             for j in range(unit // LANES):
-                await_r((i // 2) * (unit // LANES) + j).wait_recv()
+                await_r((i - units) * (unit // LANES) + j).wait_recv()
 
         together(finals_of, put_finals, lanes_of(i))
 
@@ -524,49 +524,59 @@
     pltpu.make_async_copy(rows_of_heads, rows_of_heads, line_sem).wait()
     loads[0].wait()
     loads[1].wait()
-    each(weight_step, 0, 2 * units)
+    total = 2 * units
     loads[2].wait()
-    total = 2 * units
-
-    def advance(n):
-        even_slot = lax.rem(n, 2) == 0
-
-        @pl.when(n < total)
-        def _():
-            source_step(n)
-
-        @pl.when(even_slot & (n < total))
-        def _():
-            for j in range(per_unit):
-                send_b((n // 2) * per_unit + j).start()
-
-        @pl.when(even_slot & (n >= 2))
-        def _():
-            for j in range(per_unit):
-                pair_step((n // 2 - 1) * per_unit + j)
-
-        @pl.when(even_slot & (n < total))
-        def _():
-            linear_step(n // 2)
-
-    each(advance, 0, total + 1)
+    prepared = jnp.where(lax.rem(section, 2) == 0, total // 2, total)
+    each(weight_step, 0, prepared)
 
     distance = (shards - 1 - shard) // 2
     near = distance == 1
-    relay_at = jnp.where(distance == 0, 0, jnp.where(near, 1, total))
-    early = jnp.where(not_first, 0, 1)
+    ahead = pieces // 2 * fine
+    links = pieces * fine
+
+    def advance(n):
+        source_step(n)
+
+        @pl.when(n < units)
+        def _():
+            for j in range(per_unit):
+                send_b(n * per_unit + j).start()
+
+        each(weight_step, prepared, jnp.where(n == units - 1, total, prepared))
+
+        @pl.when((n >= units - 1) & (n < total - 1))
+        def _():
+            linear_step(n - (units - 1))
+
+        each(relay_step, 0, jnp.where((n == total - 1) & near, ahead, 0))
+
+        @pl.when(n >= units)
+        def _():
+            for j in range(per_unit):
+                pair_step((n - units) * per_unit + j)
+
+    each(advance, 0, total)
+
+    each(relay_step, ahead, jnp.where(near, links, ahead))
+
+    relay_at = jnp.where(
+        distance == 0, 0, jnp.where(near, -3, jnp.where(distance == 2, total - 1, total))
+    )
+    relay_from = jnp.where(near, pieces, 0)
+    pause = jnp.where(distance == 2, total - 1, 2 * total)
+    early = jnp.where(not_first | near, 0, 1)
 
     def slot(n):
         now = n - relay_at
 
-        @pl.when((now >= 0) & (now < pieces))
+        @pl.when((now >= relay_from) & (now < pieces))
         def _():
             for j in range(fine):
                 relay_step(now * fine + j)
 
-        chosen = jnp.where(near, (n + 1) // 2, n)
-
-        @pl.when((chosen < total) & (jnp.logical_not(near) | ((n != 1) & (n != 3))))
+        chosen = n - (n > pause).astype(jnp.int32)
+
+        @pl.when((chosen < total) & (n != pause))
         def _():
             score_step(chosen)
 

time: 37.7 us -> 36.8 us (0.976)
  Pallas kernels: 36.9 us -> 36 us
    pallas_call x1, Pallas kernels: 35.6 us -> 34.7 us  [per_device(): pl.pallas_call(partial(kernel, dh, unit), in_specs=[kept] * 4 + [pl.Block...]
where the time goes in v3:
time: 36.8 us; the launch traced here: 36.7 us
  Pallas kernels  36 us (98%)
  between operations  0.64 us (2%)
    pallas_call x1, Pallas kernels, per_device(): pl.pallas_call(partial(kernel, dh, unit), in_specs=[kept] * 4 + [pl.Block...  34.7 us
    pallas_call x1, Pallas kernels, per_device(): pl.pallas_call(partial(store_kernel, heads), in_specs=[hbm] * 4, out_spec...  1.35 us

profile of v3, /device:TPU:0, one launch (start us, length us, event | category | flops | bytes accessed | tf_op | source)
XLA Modules:
  0.0 36.7 jit_solution(1628137142394237450)
XLA Ops:
  0.6 34.7 %layer_backward.1 = (bf16[128,2048]{1,0:T(8,128)(2,1)S(1)}, bf16[128,2048]{1,0:T(8,128)(2,1)S(1)}, bf16[128,2048]{1,0:T(8,128)(2,1)S(1)}, f32[1024,128]{1,0:T(8,128)S(1)}) custom-call(bf16[128,2048]{1,0:T(8,128)(2,1)} %bitcast.9, bf16[128,2048]{1,0:T(8,128)(2,1)} %bitcast.10, bf16[128,2048]{1,0:T(8,128)(2,1)} %bitcast.11, bf16[128,2048]{1,0:T(8,128)(2,1)} %bitcast.12, ...), custom_call_target="tpu_custom_call" | custom-call | tf_op jit(solution)/shard_map/layer_backward/pallas_call | solution.py:643
  35.3 1.3 %store_results.1 = (bf16[128,2048]{1,0:T(8,128)(2,1)}, bf16[128,2048]{1,0:T(8,128)(2,1)}, bf16[128,2048]{1,0:T(8,128)(2,1)}, f32[32,4096]{1,0:T(8,128)}) custom-call(bf16[128,2048]{1,0:T(8,128)(2,1)S(1)} %get-tuple-element.12.gq, bf16[128,2048]{1,0:T(8,128)(2,1)S(1)} %get-tuple-element.13.gk, bf16[128,2048]{1,0:T(8,128)(2,1)S(1)} %get-tuple-element.14.gv, ...), custom_call_target="tpu_custom_call" | custom-call | tf_op jit(solution)/shard_map/store_results/pallas_call | solution.py:665
